TPU v7x, 256 devices: a whole 4x4x8 slice. The times are simulated.
256 devices in a mesh: trial: 4 (over z_lo), ep: 4 (over y), fsdp: 16 (over z_hi, x, core).
Axes of the slice: x: 4, y: 4, z: 8 (z_hi: 2, z_lo: 4; z = z_hi * 4 + z_lo), core: 2. Of those that a mesh axis runs over, the one named last changes fastest.
Arguments:
- master_down: float32 [256, 1024, 2048], P(('trial', 'ep'), None, 'fsdp'), parts along dimension 0, may hold values from -0.25 to 0.25
- router_weight: float32 [8192, 64], P(('trial', 'fsdp'), 'ep'), parts along dimension 0, may hold values from -0.125 to 0.125
- router_gain: float32 [8192], P(('trial', 'fsdp')), parts along dimension 0, may hold values from 0.25 to 1.75
Outputs:
- final_down: bfloat16 [256, 1024, 2048], P(('trial', 'ep'), 'fsdp'), parts along dimension 0
- scale_down: float32 [256, 1024], P(('trial', 'ep'), 'fsdp'), parts along dimension 0
- serve_router: bfloat16 [8192, 64], P('trial'), parts along dimension 0
There are 4 independent parts, one for each index of `trial`. A program takes and returns all parts, laid end to end along the dimension named above; each array names one. Nothing has to cross between parts.
All inputs are finite; a program needn't handle non-finite values. Where the computation divides by a largest or mean magnitude, that divisor is 1e-20 or more.
Results may differ from a plain program's by a relative error of at most 0.001.
Values may be sent and summed in bfloat16 or wider, within the bound.
A program may use at most 64 MiB of HBM per device.

v0:
```python
import jax
import jax.numpy as jnp
from jax import lax
from jax.sharding import PartitionSpec as P


def copy_for_each(shard, axis):
    copies = jnp.broadcast_to(shard, (lax.axis_size(axis), *shard.shape))
    return lax.all_to_all(copies, axis, split_axis=0, concat_axis=0, tiled=True)


def taken_together(shard, axis):
    return copy_for_each(shard, axis).max(axis=0)


def laid_out(blocks, dim):
    lengths = list(blocks.shape[1:])
    lengths[dim] *= blocks.shape[0]
    return jnp.moveaxis(blocks, 0, dim).reshape(lengths)


def gathered_copies(shard, axis, dim):
    blocks = copy_for_each(shard, axis)
    return laid_out(blocks, dim)


def shards(master_down, router_weight, router_gain):
    scale_down = taken_together(jnp.max(jnp.abs(master_down), axis=2), "fsdp")
    narrow_down = (master_down / jnp.expand_dims(scale_down, 2)).astype(jnp.bfloat16)
    final_down = lax.all_to_all(narrow_down, "fsdp", split_axis=1, concat_axis=2, tiled=True)
    scale_down = lax.dynamic_slice_in_dim(
        scale_down, lax.axis_index("fsdp") * final_down.shape[1], final_down.shape[1], axis=1
    )
    part_router = (router_weight * router_gain[:, None]).astype(jnp.bfloat16)
    row_router = gathered_copies(part_router, "fsdp", 0)
    serve_router = lax.all_gather(row_router, "ep", axis=1, tiled=True)
    return (final_down, scale_down, serve_router)


def solution(mesh):
    return jax.shard_map(
        shards,
        mesh=mesh,
        in_specs=(
            P(("trial", "ep"), None, "fsdp"),
            P(("trial", "fsdp"), "ep"),
            P(("trial", "fsdp")),
        ),
        out_specs=(P(("trial", "ep"), "fsdp", None), P(("trial", "ep"), "fsdp"), P("trial", None)),
        check_vma=False,
    )
```

profile of v0, /device:TPU:55, one launch (start us, length us, event | category | flops | bytes accessed | tf_op | source)
XLA Modules:
  0.0 194.5 jit_solution(12414777083532193542)
XLA Ops:
  0.6 0.0 copy-start
  0.6 0.0 copy-start.1
  0.7 5.6 %abs_reduce_fusion = f32[16,1024]{1,0:T(8,128)S(1)} fusion(f32[16,1024,128]{2,1,0:T(8,128)} %param.3), kind=kLoop, calls=%fused_computation.2 | loop fusion | flops 4177920 | bytes 8454144 | tf_op jit(solution)/shard_map/reduce_max | solution.py:28
  6.3 1.1 broadcast_in_dim.8
  7.4 10.8 %all-to-all-start = ((f32[16,16,1024]{2,1,0:T(8,128)}), f32[16,16,1024]{2,1,0:T(8,128)S(1)}, u32[]{:S(2)}, u32[]{:S(2)}) async-start(f32[16,16,1024]{2,1,0:T(8,128)} %broadcast_in_dim.8), calls=%async_computation | async-start | bytes 2097152 | tf_op jit(solution)/shard_map/all_to_all | solution.py:9
  18.2 0.0 copy-done
  18.2 0.0 copy-done.1
  18.2 30.0 %all-to-all-done = f32[16,16,1024]{2,1,0:T(8,128)S(1)} async-done(((f32[16,16,1024]{2,1,0:T(8,128)}), f32[16,16,1024]{2,1,0:T(8,128)S(1)}, u32[]{:S(2)}, u32[]{:S(2)}) %all-to-all-start) | async-done | bytes 1048608 | tf_op jit(solution)/shard_map/all_to_all | solution.py:9
  48.2 0.6 broadcast_in_dim.9
  48.8 5.0 %all-to-all-start.2 = ((bf16[16,128,16]{1,2,0:T(8,128)(2,1)}), bf16[16,128,16]{1,2,0:T(8,128)(2,1)S(1)}, u32[]{:S(2)}, u32[]{:S(2)}) async-start(bf16[16,128,16]{1,2,0:T(8,128)(2,1)} %broadcast_in_dim.9), calls=%async_computation.2 | async-start | bytes 131072 | tf_op jit(solution)/shard_map/all_to_all | solution.py:9
  53.8 0.1 reduce_max.19
  53.9 0.2 copy.14
  54.1 9.6 %fusion = bf16[16,1024,128]{2,0,1:T(8,128)(2,1)} fusion(f32[16,1024,128]{2,1,0:T(8,128)} %param.3, f32[16,1024]{0,1:T(8,128)S(1)} %copy.14), kind=kLoop, calls=%fused_computation.1 | loop fusion | flops 4194304 | bytes 12648448 | tf_op jit(solution)/shard_map/convert_element_type | solution.py:29
  63.7 0.0 all-to-all-done.2
  63.7 9.7 %all-to-all-start.1 = ((bf16[16,1024,128]{2,0,1:T(8,128)(2,1)}), bf16[16,1024,128]{2,0,1:T(8,128)(2,1)}, u32[]{:S(2)}, u32[]{:S(2)}) async-start(bf16[16,1024,128]{2,0,1:T(8,128)(2,1)} %fusion), calls=%async_computation.1 | async-start | bytes 8388608 | tf_op jit(solution)/shard_map/all_to_all | solution.py:30
  73.4 9.4 %all_gather.3 = bf16[2048,64]{0,1:T(8,128)(2,1)S(1)} all-gather(bf16[2048,16]{0,1:T(8,128)(2,1)S(1)} %copy_bitcast_fusion), channel_id=1, replica_groups=mesh['trial'=4,'ep'=4,'fsdp'=16] {'ep'}, dimensions={1}, use_global_device_ids=true | all-gather | bytes 327680 | tf_op jit(solution)/shard_map/all_gather | solution.py:36
  82.7 0.7 constant_dynamic-slice_fusion
  83.4 96.2 %all-to-all-done.1 = bf16[16,1024,128]{2,0,1:T(8,128)(2,1)} async-done(((bf16[16,1024,128]{2,0,1:T(8,128)(2,1)}), bf16[16,1024,128]{2,0,1:T(8,128)(2,1)}, u32[]{:S(2)}, u32[]{:S(2)}) %all-to-all-start.1) | async-done | bytes 4194336 | tf_op jit(solution)/shard_map/all_to_all | solution.py:30
  179.7 6.9 %copy.16 = bf16[16,64,16,128]{3,2,1,0:T(8,128)(2,1)} copy(bf16[16,64,16,128]{3,0,1,2:T(8,128)(2,1)} %bitcast.1) | data formatting | bytes 8388608 | tf_op jit(solution)/shard_map/all_to_all | solution.py:30
  186.5 7.3 %all_to_all.23 = bf16[16,64,2048]{2,1,0:T(8,128)(2,1)} reshape(bf16[16,64,16,128]{3,2,1,0:T(8,128)(2,1)} %copy.16) | data formatting | bytes 8388608 | tf_op jit(solution)/shard_map/all_to_all | solution.py:30
  193.8 0.7 copy.24
  (2 shorter events, 0.0 us)
Async XLA Ops:
  0.6 17.5 %copy-start = (f32[128,16]{0,1:T(8,128)S(1)}, f32[128,16]{0,1:T(8,128)}, u32[]{:S(2)}) copy-start(f32[128,16]{0,1:T(8,128)} %param.4) | copy-start | bytes 24580
  0.6 17.5 %copy-start.1 = (f32[128]{0:T(128)S(1)}, f32[128]{0:T(128)}, u32[]{:S(2)}) copy-start(f32[128]{0:T(128)} %param.5) | copy-start | bytes 1540
  7.4 40.8 %all-to-all-start = ((f32[16,16,1024]{2,1,0:T(8,128)}), f32[16,16,1024]{2,1,0:T(8,128)S(1)}, u32[]{:S(2)}, u32[]{:S(2)}) async-start(f32[16,16,1024]{2,1,0:T(8,128)} %broadcast_in_dim.8), calls=%async_computation | async-start | bytes 2097152 | tf_op jit(solution)/shard_map/all_to_all | solution.py:9
  48.8 14.9 %all-to-all-start.2 = ((bf16[16,128,16]{1,2,0:T(8,128)(2,1)}), bf16[16,128,16]{1,2,0:T(8,128)(2,1)S(1)}, u32[]{:S(2)}, u32[]{:S(2)}) async-start(bf16[16,128,16]{1,2,0:T(8,128)(2,1)} %broadcast_in_dim.9), calls=%async_computation.2 | async-start | bytes 131072 | tf_op jit(solution)/shard_map/all_to_all | solution.py:9
  63.7 115.9 %all-to-all-start.1 = ((bf16[16,1024,128]{2,0,1:T(8,128)(2,1)}), bf16[16,1024,128]{2,0,1:T(8,128)(2,1)}, u32[]{:S(2)}, u32[]{:S(2)}) async-start(bf16[16,1024,128]{2,0,1:T(8,128)(2,1)} %fusion), calls=%async_computation.1 | async-start | bytes 8388608 | tf_op jit(solution)/shard_map/all_to_all | solution.py:30
where the time goes:
time: 195 us; the launch traced here: 194 us
  waiting for transfers between devices  126 us (65%)
  starting transfers between devices  25.5 us (13%)
  local copies, waits for them, and re-layouts  17.4 us (9%)
  other arithmetic  15.3 us (8%)
  blocking collectives  9.36 us (5%)
    all_to_all x1, waiting for transfers between devices, shards(): lax.all_to_all(narrow_down, 'fsdp', split_axis=1, concat_axis=2, tiled=True)  96.2 us
    all_to_all x2, waiting for transfers between devices, copy_for_each(): return lax.all_to_all(copies, axis, split_axis=0, concat_axis=0, tiled=True)  30 us
    all_to_all x2, starting transfers between devices, copy_for_each(): return lax.all_to_all(copies, axis, split_axis=0, concat_axis=0, tiled=True)  15.8 us
    all_to_all x2, local copies, waits for them, and re-layouts, shards(): lax.all_to_all(narrow_down, 'fsdp', split_axis=1, concat_axis=2, tiled=True)  14.1 us
    all_to_all x1, starting transfers between devices, shards(): lax.all_to_all(narrow_down, 'fsdp', split_axis=1, concat_axis=2, tiled=True)  9.66 us
    convert_element_type x1, other arithmetic, shards(): (master_down / jnp.expand_dims(scale_down, 2)).astype(jnp.bfloat16)  9.63 us
    all_gather x1, blocking collectives, shards(): serve_router = lax.all_gather(row_router, 'ep', axis=1, tiled=True)  9.36 us
    reduce_max x1, other arithmetic, shards(): scale_down = taken_together(jnp.max(jnp.abs(master_down), axis=2), 'fsdp')  5.62 us
  transfers between devices with their start and end apart: 3, of which 2 were waited for; matrix products, arithmetic and copies ran while one was open for 5% of the time, Pallas kernels for 0%

commit v1 on v0

--- a/solution.py
+++ b/solution.py
@@ -33,7 +33,9 @@
     )
     part_router = (router_weight * router_gain[:, None]).astype(jnp.bfloat16)
     row_router = gathered_copies(part_router, "fsdp", 0)
-    serve_router = lax.all_gather(row_router, "ep", axis=1, tiled=True)
+    serve_router = jnp.concatenate(
+        lax.all_to_all(jnp.stack([row_router] * lax.axis_size("ep")), "ep", 0, 0), axis=1
+    )
     return (final_down, scale_down, serve_router)
 
 

time: 195 us -> 201 us (1.031)
  waiting for transfers between devices: 126 us -> 137 us
  blocking collectives: 9.36 us -> 0 us
  starting transfers between devices: 25.5 us -> 28.7 us
    all_gather x1 -> x0, blocking collectives: 9.36 us -> none  [shards(): serve_router = lax.all_gather(row_router, 'ep', axis=1, tiled=True)]
    all_to_all x1, waiting for transfers between devices: 96.2 us -> 104 us  [shards(): lax.all_to_all(narrow_down, 'fsdp', split_axis=1, concat_axis=2, tiled=True)]
    all_to_all x0 -> x1, starting transfers between devices: none -> 4.24 us  [shards(): lax.all_to_all(jnp.stack([row_router] * lax.axis_size('ep')), 'ep', 0, 0)]
    all_to_all x1, starting transfers between devices: 9.66 us -> 6.55 us  [shards(): lax.all_to_all(narrow_down, 'fsdp', split_axis=1, concat_axis=2, tiled=True)]
    all_to_all x2, waiting for transfers between devices: 30 us -> 32.6 us  [copy_for_each(): return lax.all_to_all(copies, axis, split_axis=0, concat_axis=0, tiled=True)]
    all_to_all x2, starting transfers between devices: 15.8 us -> 17.9 us  [copy_for_each(): return lax.all_to_all(copies, axis, split_axis=0, concat_axis=0, tiled=True)]
  transfers between devices with their start and end apart: 3 -> 4, of which waited for: 2 -> 3; matrix products, arithmetic and copies ran while one was open for 5% -> 8% of each run, Pallas kernels for 0% -> 0%
where the time goes in v1:
time: 201 us; the launch traced here: 200 us
  waiting for transfers between devices  137 us (68%)
  starting transfers between devices  28.7 us (14%)
  local copies, waits for them, and re-layouts  18.2 us (9%)
  other arithmetic  16 us (8%)
    all_to_all x1, waiting for transfers between devices, shards(): lax.all_to_all(narrow_down, 'fsdp', split_axis=1, concat_axis=2, tiled=True)  104 us
    all_to_all x2, waiting for transfers between devices, copy_for_each(): return lax.all_to_all(copies, axis, split_axis=0, concat_axis=0, tiled=True)  32.6 us
    all_to_all x2, starting transfers between devices, copy_for_each(): return lax.all_to_all(copies, axis, split_axis=0, concat_axis=0, tiled=True)  17.9 us
    all_to_all x2, local copies, waits for them, and re-layouts, shards(): lax.all_to_all(narrow_down, 'fsdp', split_axis=1, concat_axis=2, tiled=True)  14.1 us
    convert_element_type x1, other arithmetic, shards(): (master_down / jnp.expand_dims(scale_down, 2)).astype(jnp.bfloat16)  9.63 us
    all_to_all x1, starting transfers between devices, shards(): lax.all_to_all(narrow_down, 'fsdp', split_axis=1, concat_axis=2, tiled=True)  6.55 us
    reduce_max x1, other arithmetic, shards(): scale_down = taken_together(jnp.max(jnp.abs(master_down), axis=2), 'fsdp')  5.61 us
    all_to_all x1, starting transfers between devices, shards(): lax.all_to_all(jnp.stack([row_router] * lax.axis_size('ep')), 'ep', 0, 0)  4.24 us
  transfers between devices with their start and end apart: 4, of which 3 were waited for; matrix products, arithmetic and copies ran while one was open for 8% of the time, Pallas kernels for 0%

profile of v1, /device:TPU:55, one launch (start us, length us, event | category | flops | bytes accessed | tf_op | source)
XLA Modules:
  0.0 200.3 jit_solution(6867620111525462243)
XLA Ops:
  0.6 0.7 multiply_convert_fusion
  1.3 0.6 broadcast_in_dim.9
  2.0 10.8 %all-to-all-start.2 = ((bf16[16,128,16]{1,2,0:T(8,128)(2,1)}), bf16[16,128,16]{1,2,0:T(8,128)(2,1)S(1)}, u32[]{:S(2)}, u32[]{:S(2)}) async-start(bf16[16,128,16]{1,2,0:T(8,128)(2,1)} %broadcast_in_dim.9), calls=%async_computation.2 | async-start | bytes 131072 | tf_op jit(solution)/shard_map/all_to_all | solution.py:9
  12.8 5.6 %abs_reduce_fusion = f32[16,1024]{1,0:T(8,128)S(1)} fusion(f32[16,1024,128]{2,1,0:T(8,128)} %param.3), kind=kLoop, calls=%fused_computation.2 | loop fusion | flops 4177920 | bytes 8454144 | tf_op jit(solution)/shard_map/reduce_max | solution.py:28
  18.4 2.6 %all-to-all-done.2 = bf16[16,128,16]{1,2,0:T(8,128)(2,1)S(1)} async-done(((bf16[16,128,16]{1,2,0:T(8,128)(2,1)}), bf16[16,128,16]{1,2,0:T(8,128)(2,1)S(1)}, u32[]{:S(2)}, u32[]{:S(2)}) %all-to-all-start.2) | async-done | bytes 65568 | tf_op jit(solution)/shard_map/all_to_all | solution.py:9
  21.0 1.1 broadcast_in_dim.8
  22.1 7.1 %all-to-all-start = ((f32[16,16,1024]{2,1,0:T(8,128)}), f32[16,16,1024]{2,1,0:T(8,128)S(1)}, u32[]{:S(2)}, u32[]{:S(2)}) async-start(f32[16,16,1024]{2,1,0:T(8,128)} %broadcast_in_dim.8), calls=%async_computation | async-start | bytes 2097152 | tf_op jit(solution)/shard_map/all_to_all | solution.py:9
  29.1 30.0 %all-to-all-done = f32[16,16,1024]{2,1,0:T(8,128)S(1)} async-done(((f32[16,16,1024]{2,1,0:T(8,128)}), f32[16,16,1024]{2,1,0:T(8,128)S(1)}, u32[]{:S(2)}, u32[]{:S(2)}) %all-to-all-start) | async-done | bytes 1048608 | tf_op jit(solution)/shard_map/all_to_all | solution.py:9
  59.1 0.7 stack.3
  59.8 4.2 %all-to-all-start.3 = ((bf16[4,2048,16]{1,2,0:T(8,128)(2,1)}), bf16[4,2048,16]{1,2,0:T(8,128)(2,1)S(1)}, u32[]{:S(2)}, u32[]{:S(2)}) async-start(bf16[4,2048,16]{1,2,0:T(8,128)(2,1)} %stack.3), calls=%async_computation.3 | async-start | bytes 524288 | tf_op jit(solution)/shard_map/all_to_all | solution.py:37
  64.1 0.1 reduce_max.19
  64.1 0.2 copy.14
  64.3 9.6 %fusion = bf16[16,1024,128]{2,0,1:T(8,128)(2,1)} fusion(f32[16,1024,128]{2,1,0:T(8,128)} %param.3, f32[16,1024]{0,1:T(8,128)S(1)} %copy.14), kind=kLoop, calls=%fused_computation.1 | loop fusion | flops 4194304 | bytes 12648448 | tf_op jit(solution)/shard_map/convert_element_type | solution.py:29
  74.0 0.0 all-to-all-done.3
  74.0 6.5 %all-to-all-start.1 = ((bf16[16,1024,128]{2,0,1:T(8,128)(2,1)}), bf16[16,1024,128]{2,0,1:T(8,128)(2,1)}, u32[]{:S(2)}, u32[]{:S(2)}) async-start(bf16[16,1024,128]{2,0,1:T(8,128)(2,1)} %fusion), calls=%async_computation.1 | async-start | bytes 8388608 | tf_op jit(solution)/shard_map/all_to_all | solution.py:30
  80.5 0.7 constant_dynamic-slice_fusion
  81.2 104.3 %all-to-all-done.1 = bf16[16,1024,128]{2,0,1:T(8,128)(2,1)} async-done(((bf16[16,1024,128]{2,0,1:T(8,128)(2,1)}), bf16[16,1024,128]{2,0,1:T(8,128)(2,1)}, u32[]{:S(2)}, u32[]{:S(2)}) %all-to-all-start.1) | async-done | bytes 4194336 | tf_op jit(solution)/shard_map/all_to_all | solution.py:30
  185.5 6.9 %copy.16 = bf16[16,64,16,128]{3,2,1,0:T(8,128)(2,1)} copy(bf16[16,64,16,128]{3,0,1,2:T(8,128)(2,1)} %bitcast.1) | data formatting | bytes 8388608 | tf_op jit(solution)/shard_map/all_to_all | solution.py:30
  192.4 7.3 %all_to_all.26 = bf16[16,64,2048]{2,1,0:T(8,128)(2,1)} reshape(bf16[16,64,16,128]{3,2,1,0:T(8,128)(2,1)} %copy.16) | data formatting | bytes 8388608 | tf_op jit(solution)/shard_map/all_to_all | solution.py:30
  199.6 0.7 copy.24
  (1 shorter events, 0.0 us)
Async XLA Ops:
  2.0 19.0 %all-to-all-start.2 = ((bf16[16,128,16]{1,2,0:T(8,128)(2,1)}), bf16[16,128,16]{1,2,0:T(8,128)(2,1)S(1)}, u32[]{:S(2)}, u32[]{:S(2)}) async-start(bf16[16,128,16]{1,2,0:T(8,128)(2,1)} %broadcast_in_dim.9), calls=%async_computation.2 | async-start | bytes 131072 | tf_op jit(solution)/shard_map/all_to_all | solution.py:9
  22.1 37.1 %all-to-all-start = ((f32[16,16,1024]{2,1,0:T(8,128)}), f32[16,16,1024]{2,1,0:T(8,128)S(1)}, u32[]{:S(2)}, u32[]{:S(2)}) async-start(f32[16,16,1024]{2,1,0:T(8,128)} %broadcast_in_dim.8), calls=%async_computation | async-start | bytes 2097152 | tf_op jit(solution)/shard_map/all_to_all | solution.py:9
  59.8 14.1 %all-to-all-start.3 = ((bf16[4,2048,16]{1,2,0:T(8,128)(2,1)}), bf16[4,2048,16]{1,2,0:T(8,128)(2,1)S(1)}, u32[]{:S(2)}, u32[]{:S(2)}) async-start(bf16[4,2048,16]{1,2,0:T(8,128)(2,1)} %stack.3), calls=%async_computation.3 | async-start | bytes 524288 | tf_op jit(solution)/shard_map/all_to_all | solution.py:37
  74.0 111.5 %all-to-all-start.1 = ((bf16[16,1024,128]{2,0,1:T(8,128)(2,1)}), bf16[16,1024,128]{2,0,1:T(8,128)(2,1)}, u32[]{:S(2)}, u32[]{:S(2)}) async-start(bf16[16,1024,128]{2,0,1:T(8,128)(2,1)} %fusion), calls=%async_computation.1 | async-start | bytes 8388608 | tf_op jit(solution)/shard_map/all_to_all | solution.py:30
